TPU v7x, 512 devices: a 4x2x32 block of a 4x8x32 slice. The times are simulated.
512 devices in a mesh: groups: 2 (over y), row: 32 (over z), col: 4 (over x), rep: 2 (over core).
Axes of the slice: x: 4, y: 2, z: 32, core: 2. Of those that a mesh axis runs over, the one named last changes fastest.
The devices are a block of a 4x8x32 slice.
Arguments:
- kernel: float32 [32768, 16384], P(('groups', 'row'), ('col', 'rep')), parts along dimension 0, may hold values from 0 to 2, as said below
- source: float32 [64, 16384], P('groups', 'row'), parts along dimension 0, may hold values from 0.5 to 2, as said below
- target: float32 [64, 16384], P('groups', ('col', 'rep')), parts along dimension 0, may hold values from 0.5 to 2, as said below
Outputs:
- left_scale: float32 [64, 16384], P('groups', 'row'), parts along dimension 0
- right_scale: float32 [64, 16384], P('groups', ('col', 'rep')), parts along dimension 0
- errors: float32 [6, 32], P('groups'), parts along dimension 0
There are 2 independent parts, one for each index of `groups`. A program takes and returns all parts, laid end to end along the dimension named above; each array names one. Nothing has to cross between parts.
Inputs may be any that keep to these rules, and one draw needn't show every extreme that they name: `kernel`: every entry is positive. `source`: every entry is positive. `target`: every entry is positive.
All inputs are finite; a program needn't handle non-finite values.
Results may differ from a plain program's by a relative error of at most 0.0001.
Values sent between devices are 32-bit elements; how exact they have to be, the bound alone decides.
No kernel may reach another device: no remote copies, remote signals or barrier semaphores. Data moves between devices by JAX's collectives and lax.ppermute only.
A program may use at most 64 MiB of HBM per device.

v0:
```python
import jax
import jax.numpy as jnp
from jax import lax
from jax.sharding import PartitionSpec as P

N = 16384
ITERS = 3


def from_everyone(array, axis):
    copies = jnp.broadcast_to(array, (lax.axis_size(axis), *array.shape))
    return lax.all_to_all(copies, axis, split_axis=0, concat_axis=0, tiled=True)


def over_copies(array, axis):
    everything = from_everyone(array, axis)
    return jnp.sum(everything, axis=0)


def in_blocks(array, dim, length):
    shape = array.shape
    pieces = array.reshape(*shape[:dim], length, shape[dim] // length, *shape[dim + 1 :])
    return jnp.moveaxis(pieces, dim, 0)


def sent_and_summed(array, axis, dim):
    pieces = in_blocks(array, dim, lax.axis_size(axis))
    arrived = lax.all_to_all(pieces, axis, split_axis=0, concat_axis=0, tiled=True)
    return arrived.sum(axis=0)


def laid_out(pieces, dim):
    pieces = jnp.moveaxis(pieces, 0, dim)
    shape = pieces.shape
    return pieces.reshape(*shape[:dim], shape[dim] * shape[dim + 1], *shape[dim + 2 :])


def collect(array, axis, dim):
    pieces = from_everyone(array, axis)
    return laid_out(pieces, dim)


def by_axis(array, axes):
    for axis in axes:
        array = lax.psum(array, axis)
    return array


def local(kernel, source, target):
    columns = kernel.shape[1]
    right_scale = jnp.ones(target.shape, jnp.float32)
    left_scale = source
    share = columns // lax.axis_size("row")
    offset = lax.axis_index("row") * share
    terms = []
    for step in range(ITERS):
        partial_value = lax.dot_general(
            right_scale, kernel, (((1,), (1,)), ((), ())), precision=lax.Precision.HIGHEST
        )
        left_scale = source / over_copies(partial_value, ("col", "rep"))
        back = jnp.dot(left_scale, kernel, precision=lax.Precision.HIGHEST)
        old_piece = lax.dynamic_slice_in_dim(right_scale, offset, share, 1)
        target_piece = lax.dynamic_slice_in_dim(target, offset, share, 1)
        total_piece = sent_and_summed(back, "row", 1)
        right_scale = collect(target_piece / total_piece, "row", 1)
        term = jnp.sum(jnp.abs(old_piece * total_piece - target_piece), axis=1) / N
        terms.append(term)
    stacked = by_axis(jnp.stack(terms), ("row", "col", "rep"))
    return (left_scale, right_scale, stacked)


def solution(mesh):
    return jax.shard_map(
        local,
        mesh=mesh,
        in_specs=(
            P(("groups", "row"), ("col", "rep")),
            P("groups", "row"),
            P("groups", ("col", "rep")),
        ),
        out_specs=(P("groups", "row"), P("groups", ("col", "rep")), P("groups", None)),
        check_vma=False,
    )
```

profile of v0, /device:TPU:33, one launch (start us, length us, event | category | flops | bytes accessed | tf_op | source)
XLA Modules:
  0.0 451.9 jit_solution(4674217970748007036)
XLA Ops:
  0.6 6.0 %fusion = f32[32,512]{1,0:T(8,128)S(1)} fusion(f32[512,2048]{1,0:T(8,128)} %param.3), kind=kOutput, calls=%fused_computation.3 | convolution fusion | flops 402653184 | bytes 4259840 | tf_op jit(solution)/shard_map/dot_general | solution.py:57
  6.7 0.1 broadcast_in_dim.22
  6.8 53.2 %all_to_all.45 = f32[8,32,512]{2,1,0:T(8,128)S(1)} all-to-all(f32[8,32,512]{2,1,0:T(8,128)S(1)} %broadcast_in_dim.22), channel_id=1, replica_groups=mesh['groups'=2,'row'=32,'col'=4,'rep'=2] {'col','rep'}, dimensions={0} | all-to-all | bytes 1048576 | tf_op jit(solution)/shard_map/all_to_all | solution.py:12
  60.0 4.7 %fusion.4 = f32[32,2048]{1,0:T(8,128)S(1)} fusion(f32[512,2048]{1,0:T(8,128)} %param.3, f32[32,512]{1,0:T(8,128)S(1)} %copy-done, f32[32,512]{1,0:T(8,128)S(1)} %reduce_sum.81), kind=kOutput, calls=%fused_computation.7 | convolution fusion | flops 402669568 | bytes 4587520 | tf_op jit(solution)/shard_map/dot_general | solution.py:61
  64.7 0.2 reshape.51
  65.0 0.3 copy.26
  65.3 1.0 reshape.57
  66.3 7.4 %all-to-all-start.1 = ((f32[32,1,2048]{2,1,0:T(1,128)}), f32[32,1,2048]{2,1,0:T(1,128)S(1)}, u32[]{:S(2)}, u32[]{:S(2)}) async-start(f32[32,1,2048]{2,1,0:T(1,128)} %reshape.57), calls=%async_computation.1 | async-start | bytes 524288 | tf_op jit(solution)/shard_map/all_to_all | solution.py:28
  73.7 40.0 %all-to-all-done.1 = f32[32,1,2048]{2,1,0:T(1,128)S(1)} async-done(((f32[32,1,2048]{2,1,0:T(1,128)}), f32[32,1,2048]{2,1,0:T(1,128)S(1)}, u32[]{:S(2)}, u32[]{:S(2)}) %all-to-all-start.1) | async-done | bytes 262176 | tf_op jit(solution)/shard_map/all_to_all | solution.py:28
  113.7 0.6 broadcast.35
  114.3 1.3 reduce
  115.6 0.2 reshape.58
  115.8 0.1 reduce_sum.82
  115.9 0.8 dynamic-slice_divide_fusion.2
  116.7 0.1 broadcast_in_dim.23
  116.7 0.3 reshape.59
  117.1 42.2 %all_to_all.46 = f32[32,1,2048]{2,1,0:T(1,128)S(1)} all-to-all(f32[32,1,2048]{2,1,0:T(1,128)S(1)} %reshape.59), channel_id=1, replica_groups=mesh['groups'=2,'row'=32,'col'=4,'rep'=2] {'row'}, dimensions={0} | all-to-all | bytes 524288 | tf_op jit(solution)/shard_map/all_to_all | solution.py:12
  159.2 1.3 reduce.1
  160.5 0.2 reshape.60
  160.8 0.3 copy.16
  161.1 0.2 reshape.52
  161.3 6.0 %fusion.7 = f32[32,512]{1,0:T(8,128)S(1)} fusion(f32[32,2048]{1,0:T(8,128)S(1)} %reshape.52, f32[512,2048]{1,0:T(8,128)} %param.3), kind=kOutput, calls=%fused_computation.20 | convolution fusion | flops 402653184 | bytes 4521984 | tf_op jit(solution)/shard_map/dot_general | solution.py:57
  167.3 0.1 broadcast_in_dim.24
  167.3 17.1 %all_to_all.47 = f32[8,32,512]{2,1,0:T(8,128)S(1)} all-to-all(f32[8,32,512]{2,1,0:T(8,128)S(1)} %broadcast_in_dim.24), channel_id=1, replica_groups=mesh['groups'=2,'row'=32,'col'=4,'rep'=2] {'col','rep'}, dimensions={0} | all-to-all | bytes 1048576 | tf_op jit(solution)/shard_map/all_to_all | solution.py:12
  184.5 4.7 %fusion.2 = f32[32,2048]{1,0:T(8,128)S(1)} fusion(f32[512,2048]{1,0:T(8,128)} %param.3, f32[32,512]{1,0:T(8,128)S(1)} %copy-done, f32[32,512]{1,0:T(8,128)S(1)} %reduce_sum.83), kind=kOutput, calls=%fused_computation.5 | convolution fusion | flops 402669568 | bytes 4587520 | tf_op jit(solution)/shard_map/dot_general | solution.py:61
  189.2 0.2 reshape.53
  189.4 0.3 copy.25
  189.7 0.3 reshape.61
  190.0 43.4 %all_to_all.48 = f32[32,1,2048]{2,1,0:T(1,128)S(1)} all-to-all(f32[32,1,2048]{2,1,0:T(1,128)S(1)} %reshape.61), channel_id=1, replica_groups=mesh['groups'=2,'row'=32,'col'=4,'rep'=2] {'row'}, dimensions={0} | all-to-all | bytes 524288 | tf_op jit(solution)/shard_map/all_to_all | solution.py:28
  233.4 1.3 reduce.2
  234.7 0.2 reshape.62
  234.9 0.1 reduce_sum.84
  235.0 0.8 dynamic-slice_divide_fusion.1
  235.8 0.1 broadcast_in_dim.25
  235.9 0.3 reshape.63
  236.2 42.6 %all_to_all.49 = f32[32,1,2048]{2,1,0:T(1,128)S(1)} all-to-all(f32[32,1,2048]{2,1,0:T(1,128)S(1)} %reshape.63), channel_id=1, replica_groups=mesh['groups'=2,'row'=32,'col'=4,'rep'=2] {'row'}, dimensions={0} | all-to-all | bytes 524288 | tf_op jit(solution)/shard_map/all_to_all | solution.py:12
  278.8 1.3 reduce.3
  280.1 0.2 reshape.64
  280.4 0.3 copy.18
  280.7 0.2 reshape.54
  280.9 6.0 %fusion.8 = f32[32,512]{1,0:T(8,128)S(1)} fusion(f32[32,2048]{1,0:T(8,128)S(1)} %reshape.54, f32[512,2048]{1,0:T(8,128)} %param.3), kind=kOutput, calls=%fused_computation.21 | convolution fusion | flops 402653184 | bytes 4521984 | tf_op jit(solution)/shard_map/dot_general | solution.py:57
  286.9 0.1 broadcast_in_dim.26
  286.9 17.1 %all_to_all.50 = f32[8,32,512]{2,1,0:T(8,128)S(1)} all-to-all(f32[8,32,512]{2,1,0:T(8,128)S(1)} %broadcast_in_dim.26), channel_id=1, replica_groups=mesh['groups'=2,'row'=32,'col'=4,'rep'=2] {'col','rep'}, dimensions={0} | all-to-all | bytes 1048576 | tf_op jit(solution)/shard_map/all_to_all | solution.py:12
  304.1 0.0 copy-start.1
  304.2 4.7 %fusion.9 = f32[32,2048]{1,0:T(8,128)S(1)} fusion(f32[32,512]{1,0:T(8,128)S(1)} %div.37, f32[512,2048]{1,0:T(8,128)} %param.3), kind=kOutput, calls=%fused_computation.22 | convolution fusion | flops 402653184 | bytes 4521984 | tf_op jit(solution)/shard_map/dot_general | solution.py:61
  308.9 0.2 reshape.55
  309.1 0.3 copy.24
  309.4 0.3 reshape.65
  309.7 43.4 %all_to_all.51 = f32[32,1,2048]{2,1,0:T(1,128)S(1)} all-to-all(f32[32,1,2048]{2,1,0:T(1,128)S(1)} %reshape.65), channel_id=1, replica_groups=mesh['groups'=2,'row'=32,'col'=4,'rep'=2] {'row'}, dimensions={0} | all-to-all | bytes 524288 | tf_op jit(solution)/shard_map/all_to_all | solution.py:28
  353.1 1.3 reduce.4
  354.4 0.2 reshape.66
  354.6 0.1 reduce_sum.86
  354.7 1.0 abs_reduce_fusion.2
  355.6 0.1 broadcast_in_dim.27
  355.7 1.0 reshape.67
  356.7 5.2 %all-to-all-start.8 = ((f32[32,1,2048]{2,1,0:T(1,128)}), f32[32,1,2048]{2,1,0:T(1,128)S(1)}, u32[]{:S(2)}, u32[]{:S(2)}) async-start(f32[32,1,2048]{2,1,0:T(1,128)} %reshape.67), calls=%async_computation.8 | async-start | bytes 524288 | tf_op jit(solution)/shard_map/all_to_all | solution.py:12
  362.0 61.2 %psum.21 = f32[3,32]{1,0:T(4,128)S(1)} all-reduce(f32[3,32]{1,0:T(4,128)S(1)} %pad_maximum_fusion), channel_id=1, replica_groups=mesh['groups'=2,'row'=32,'col'=4,'rep'=2] {'row'}, use_global_device_ids=true, to_apply=%region_9.0 | all-reduce | flops 96 | bytes 768 | tf_op jit(solution)/shard_map/psum | solution.py:45
  423.2 6.9 %psum.22 = f32[3,32]{1,0:T(4,128)S(1)} all-reduce(f32[3,32]{1,0:T(4,128)S(1)} %psum.21), channel_id=1, replica_groups=mesh['groups'=2,'row'=32,'col'=4,'rep'=2] {'col'}, use_global_device_ids=true, to_apply=%region_10.0 | all-reduce | flops 96 | bytes 768 | tf_op jit(solution)/shard_map/psum | solution.py:45
  430.1 19.1 %psum.23 = f32[3,32]{1,0:T(4,128)} all-reduce(f32[3,32]{1,0:T(4,128)S(1)} %psum.22), channel_id=1, replica_groups=mesh['groups'=2,'row'=32,'col'=4,'rep'=2] {'rep'}, use_global_device_ids=true, to_apply=%region_11.0 | all-reduce | flops 96 | bytes 768 | tf_op jit(solution)/shard_map/psum | solution.py:45
  449.1 0.0 all-to-all-done.8
  449.2 1.3 reduce.5
  450.5 0.2 reshape.68
  450.7 0.3 copy.20
  451.0 0.9 reshape.56
  (10 shorter events, 0.2 us)
Async XLA Ops:
  0.6 59.4 %copy-start = (f32[32,512]{1,0:T(8,128)S(1)}, f32[32,512]{1,0:T(8,128)}, u32[]{:S(2)}) copy-start(f32[32,512]{1,0:T(8,128)} %param.4) | copy-start | bytes 196612
  66.3 47.4 %all-to-all-start.1 = ((f32[32,1,2048]{2,1,0:T(1,128)}), f32[32,1,2048]{2,1,0:T(1,128)S(1)}, u32[]{:S(2)}, u32[]{:S(2)}) async-start(f32[32,1,2048]{2,1,0:T(1,128)} %reshape.57), calls=%async_computation.1 | async-start | bytes 524288 | tf_op jit(solution)/shard_map/all_to_all | solution.py:28
  304.1 50.5 %copy-start.1 = (f32[32,512]{1,0:T(8,128)}, f32[32,512]{1,0:T(8,128)S(1)}, u32[]{:S(2)}) copy-start(f32[32,512]{1,0:T(8,128)S(1)} %div.37) | copy-start | bytes 196612
  356.7 92.4 %all-to-all-start.8 = ((f32[32,1,2048]{2,1,0:T(1,128)}), f32[32,1,2048]{2,1,0:T(1,128)S(1)}, u32[]{:S(2)}, u32[]{:S(2)}) async-start(f32[32,1,2048]{2,1,0:T(1,128)} %reshape.67), calls=%async_computation.8 | async-start | bytes 524288 | tf_op jit(solution)/shard_map/all_to_all | solution.py:12
where the time goes:
time: 453 us; the launch traced here: 452 us
  blocking collectives  346 us (76%)
  waiting for transfers between devices  40 us (9%)
  matrix products  32.1 us (7%)
  starting transfers between devices  12.5 us (3%)
  other arithmetic  10.7 us (2%)
  local copies, waits for them, and re-layouts  9.31 us (2%)
    all_to_all x5, blocking collectives, from_everyone(): return lax.all_to_all(copies, axis, split_axis=0, concat_axis=0, tiled=True)  172 us
    psum x3, blocking collectives, by_axis(): array = lax.psum(array, axis)  87.2 us
    all_to_all x2, blocking collectives, sent_and_summed(): lax.all_to_all(pieces, axis, split_axis=0, concat_axis=0, tiled=True)  86.8 us
    all_to_all x1, waiting for transfers between devices, sent_and_summed(): lax.all_to_all(pieces, axis, split_axis=0, concat_axis=0, tiled=True)  40 us
    dot_general x3, matrix products, local(): lax.dot_general(right_scale, kernel, (((1,), (1,)), ((), ())), precision=...  18.1 us
    dot_general x3, matrix products, local(): back = jnp.dot(left_scale, kernel, precision=lax.Precision.HIGHEST)  14 us
  transfers between devices with their start and end apart: 2, of which 1 were waited for; matrix products, arithmetic and copies ran while one was open for 0% of the time, Pallas kernels for 0%

commit v1 on v0

--- a/solution.py
+++ b/solution.py
@@ -42,7 +42,7 @@
 
 def by_axis(array, axes):
     for axis in axes:
-        array = lax.psum(array, axis)
+        array = jnp.sum(lax.all_gather(array, axis), axis=0)
     return array
 
 

time: 453 us -> 453 us (level)
    psum x3 -> x0, blocking collectives: 87.2 us -> none  [by_axis(): array = lax.psum(array, axis)]
    all_gather x0 -> x3, blocking collectives: none -> 87 us  [by_axis(): array = jnp.sum(lax.all_gather(array, axis), axis=0)]
where the time goes in v1:
time: 453 us; the launch traced here: 452 us
  blocking collectives  346 us (76%)
  waiting for transfers between devices  40 us (9%)
  matrix products  32.1 us (7%)
  starting transfers between devices  12.5 us (3%)
  other arithmetic  11.3 us (2%)
  local copies, waits for them, and re-layouts  9.31 us (2%)
    all_to_all x5, blocking collectives, from_everyone(): return lax.all_to_all(copies, axis, split_axis=0, concat_axis=0, tiled=True)  172 us
    all_gather x3, blocking collectives, by_axis(): array = jnp.sum(lax.all_gather(array, axis), axis=0)  87 us
    all_to_all x2, blocking collectives, sent_and_summed(): lax.all_to_all(pieces, axis, split_axis=0, concat_axis=0, tiled=True)  86.8 us
    all_to_all x1, waiting for transfers between devices, sent_and_summed(): lax.all_to_all(pieces, axis, split_axis=0, concat_axis=0, tiled=True)  40 us
    dot_general x3, matrix products, local(): lax.dot_general(right_scale, kernel, (((1,), (1,)), ((), ())), precision=...  18.1 us
    dot_general x3, matrix products, local(): back = jnp.dot(left_scale, kernel, precision=lax.Precision.HIGHEST)  14 us
  transfers between devices with their start and end apart: 2, of which 1 were waited for; matrix products, arithmetic and copies ran while one was open for 0% of the time, Pallas kernels for 0%

profile of v1, /device:TPU:33, one launch (start us, length us, event | category | flops | bytes accessed | tf_op | source)
XLA Modules:
  0.0 452.3 jit_solution(905105323771229151)
XLA Ops:
  0.6 6.0 %fusion = f32[32,512]{1,0:T(8,128)S(1)} fusion(f32[512,2048]{1,0:T(8,128)} %param.3), kind=kOutput, calls=%fused_computation.3 | convolution fusion | flops 402653184 | bytes 4259840 | tf_op jit(solution)/shard_map/dot_general | solution.py:57
  6.7 0.1 broadcast_in_dim.22
  6.8 53.2 %all_to_all.45 = f32[8,32,512]{2,1,0:T(8,128)S(1)} all-to-all(f32[8,32,512]{2,1,0:T(8,128)S(1)} %broadcast_in_dim.22), channel_id=1, replica_groups=mesh['groups'=2,'row'=32,'col'=4,'rep'=2] {'col','rep'}, dimensions={0} | all-to-all | bytes 1048576 | tf_op jit(solution)/shard_map/all_to_all | solution.py:12
  60.0 4.7 %fusion.4 = f32[32,2048]{1,0:T(8,128)S(1)} fusion(f32[512,2048]{1,0:T(8,128)} %param.3, f32[32,512]{1,0:T(8,128)S(1)} %copy-done, f32[32,512]{1,0:T(8,128)S(1)} %reduce_sum.108), kind=kOutput, calls=%fused_computation.7 | convolution fusion | flops 402669568 | bytes 4587520 | tf_op jit(solution)/shard_map/dot_general | solution.py:61
  64.7 0.2 reshape.51
  65.0 0.3 copy.26
  65.3 1.0 reshape.69
  66.3 7.4 %all-to-all-start.1 = ((f32[32,1,2048]{2,1,0:T(1,128)}), f32[32,1,2048]{2,1,0:T(1,128)S(1)}, u32[]{:S(2)}, u32[]{:S(2)}) async-start(f32[32,1,2048]{2,1,0:T(1,128)} %reshape.69), calls=%async_computation.1 | async-start | bytes 524288 | tf_op jit(solution)/shard_map/all_to_all | solution.py:28
  73.7 40.0 %all-to-all-done.1 = f32[32,1,2048]{2,1,0:T(1,128)S(1)} async-done(((f32[32,1,2048]{2,1,0:T(1,128)}), f32[32,1,2048]{2,1,0:T(1,128)S(1)}, u32[]{:S(2)}, u32[]{:S(2)}) %all-to-all-start.1) | async-done | bytes 262176 | tf_op jit(solution)/shard_map/all_to_all | solution.py:28
  113.7 0.6 broadcast.35
  114.3 1.3 reduce.3
  115.6 0.2 reshape.70
  115.8 0.1 reduce_sum.109
  115.9 0.8 dynamic-slice_divide_fusion.2
  116.7 0.1 broadcast_in_dim.23
  116.7 0.3 reshape.71
  117.1 42.2 %all_to_all.46 = f32[32,1,2048]{2,1,0:T(1,128)S(1)} all-to-all(f32[32,1,2048]{2,1,0:T(1,128)S(1)} %reshape.71), channel_id=1, replica_groups=mesh['groups'=2,'row'=32,'col'=4,'rep'=2] {'row'}, dimensions={0} | all-to-all | bytes 524288 | tf_op jit(solution)/shard_map/all_to_all | solution.py:12
  159.2 1.3 reduce.4
  160.5 0.2 reshape.72
  160.7 0.3 copy.16
  161.1 0.2 reshape.52
  161.2 6.0 %fusion.7 = f32[32,512]{1,0:T(8,128)S(1)} fusion(f32[32,2048]{1,0:T(8,128)S(1)} %reshape.52, f32[512,2048]{1,0:T(8,128)} %param.3), kind=kOutput, calls=%fused_computation.20 | convolution fusion | flops 402653184 | bytes 4521984 | tf_op jit(solution)/shard_map/dot_general | solution.py:57
  167.3 0.1 broadcast_in_dim.24
  167.3 17.1 %all_to_all.47 = f32[8,32,512]{2,1,0:T(8,128)S(1)} all-to-all(f32[8,32,512]{2,1,0:T(8,128)S(1)} %broadcast_in_dim.24), channel_id=1, replica_groups=mesh['groups'=2,'row'=32,'col'=4,'rep'=2] {'col','rep'}, dimensions={0} | all-to-all | bytes 1048576 | tf_op jit(solution)/shard_map/all_to_all | solution.py:12
  184.5 4.7 %fusion.2 = f32[32,2048]{1,0:T(8,128)S(1)} fusion(f32[512,2048]{1,0:T(8,128)} %param.3, f32[32,512]{1,0:T(8,128)S(1)} %copy-done, f32[32,512]{1,0:T(8,128)S(1)} %reduce_sum.110), kind=kOutput, calls=%fused_computation.5 | convolution fusion | flops 402669568 | bytes 4587520 | tf_op jit(solution)/shard_map/dot_general | solution.py:61
  189.2 0.2 reshape.53
  189.4 0.3 copy.25
  189.7 0.3 reshape.73
  190.0 43.4 %all_to_all.48 = f32[32,1,2048]{2,1,0:T(1,128)S(1)} all-to-all(f32[32,1,2048]{2,1,0:T(1,128)S(1)} %reshape.73), channel_id=1, replica_groups=mesh['groups'=2,'row'=32,'col'=4,'rep'=2] {'row'}, dimensions={0} | all-to-all | bytes 524288 | tf_op jit(solution)/shard_map/all_to_all | solution.py:28
  233.4 1.3 reduce.5
  234.7 0.2 reshape.74
  234.9 0.1 reduce_sum.111
  235.0 0.8 dynamic-slice_divide_fusion.1
  235.8 0.1 broadcast_in_dim.25
  235.8 0.3 reshape.75
  236.2 42.6 %all_to_all.49 = f32[32,1,2048]{2,1,0:T(1,128)S(1)} all-to-all(f32[32,1,2048]{2,1,0:T(1,128)S(1)} %reshape.75), channel_id=1, replica_groups=mesh['groups'=2,'row'=32,'col'=4,'rep'=2] {'row'}, dimensions={0} | all-to-all | bytes 524288 | tf_op jit(solution)/shard_map/all_to_all | solution.py:12
  278.8 1.3 reduce.6
  280.1 0.2 reshape.76
  280.4 0.3 copy.18
  280.7 0.2 reshape.54
  280.9 6.0 %fusion.8 = f32[32,512]{1,0:T(8,128)S(1)} fusion(f32[32,2048]{1,0:T(8,128)S(1)} %reshape.54, f32[512,2048]{1,0:T(8,128)} %param.3), kind=kOutput, calls=%fused_computation.21 | convolution fusion | flops 402653184 | bytes 4521984 | tf_op jit(solution)/shard_map/dot_general | solution.py:57
  286.9 0.1 broadcast_in_dim.26
  286.9 17.1 %all_to_all.50 = f32[8,32,512]{2,1,0:T(8,128)S(1)} all-to-all(f32[8,32,512]{2,1,0:T(8,128)S(1)} %broadcast_in_dim.26), channel_id=1, replica_groups=mesh['groups'=2,'row'=32,'col'=4,'rep'=2] {'col','rep'}, dimensions={0} | all-to-all | bytes 1048576 | tf_op jit(solution)/shard_map/all_to_all | solution.py:12
  304.1 0.0 copy-start.1
  304.1 4.7 %fusion.9 = f32[32,2048]{1,0:T(8,128)S(1)} fusion(f32[32,512]{1,0:T(8,128)S(1)} %div.37, f32[512,2048]{1,0:T(8,128)} %param.3), kind=kOutput, calls=%fused_computation.22 | convolution fusion | flops 402653184 | bytes 4521984 | tf_op jit(solution)/shard_map/dot_general | solution.py:61
  308.8 0.2 reshape.55
  309.1 0.3 copy.24
  309.4 0.3 reshape.77
  309.7 43.4 %all_to_all.51 = f32[32,1,2048]{2,1,0:T(1,128)S(1)} all-to-all(f32[32,1,2048]{2,1,0:T(1,128)S(1)} %reshape.77), channel_id=1, replica_groups=mesh['groups'=2,'row'=32,'col'=4,'rep'=2] {'row'}, dimensions={0} | all-to-all | bytes 524288 | tf_op jit(solution)/shard_map/all_to_all | solution.py:28
  353.1 1.3 reduce.7
  354.4 0.2 reshape.78
  354.6 0.1 reduce_sum.113
  354.7 1.0 abs_reduce_fusion.2
  355.6 0.1 broadcast_in_dim.27
  355.7 1.0 reshape.79
  356.7 5.2 %all-to-all-start.8 = ((f32[32,1,2048]{2,1,0:T(1,128)}), f32[32,1,2048]{2,1,0:T(1,128)S(1)}, u32[]{:S(2)}, u32[]{:S(2)}) async-start(f32[32,1,2048]{2,1,0:T(1,128)} %reshape.79), calls=%async_computation.8 | async-start | bytes 524288 | tf_op jit(solution)/shard_map/all_to_all | solution.py:12
  362.0 60.3 %all-gather.3 = f32[32,3,32]{2,1,0:T(4,128)S(1)} all-gather(f32[1,3,32]{2,1,0:T(4,128)S(1)} %maximum_bitcast_fusion), channel_id=2, replica_groups=mesh['groups'=2,'row'=32,'col'=4,'rep'=2] {'row'}, dimensions={0}, use_global_device_ids=true | all-gather | bytes 12672 | tf_op jit(solution)/shard_map/all_gather | solution.py:45
  422.3 8.5 %all-gather.4 = f32[4,3,32]{2,1,0:T(4,128)S(1)} all-gather(f32[1,3,32]{2,1,0:T(4,128)S(1)} %bitcast.37), channel_id=3, replica_groups=mesh['groups'=2,'row'=32,'col'=4,'rep'=2] {'col'}, dimensions={0}, use_global_device_ids=true | all-gather | bytes 1920 | tf_op jit(solution)/shard_map/all_gather | solution.py:45
  430.8 18.2 %all-gather.5 = f32[2,3,32]{2,1,0:T(4,128)S(1)} all-gather(f32[1,3,32]{2,1,0:T(4,128)S(1)} %bitcast.38), channel_id=4, replica_groups=mesh['groups'=2,'row'=32,'col'=4,'rep'=2] {'rep'}, dimensions={0}, use_global_device_ids=true | all-gather | bytes 1152 | tf_op jit(solution)/shard_map/all_gather | solution.py:45
  449.0 0.6 reduce_sum.119
  449.6 1.3 reduce.8
  450.9 0.2 reshape.80
  451.1 0.3 copy.20
  451.4 0.9 reshape.56
  (13 shorter events, 0.2 us)
Async XLA Ops:
  0.6 59.4 %copy-start = (f32[32,512]{1,0:T(8,128)S(1)}, f32[32,512]{1,0:T(8,128)}, u32[]{:S(2)}) copy-start(f32[32,512]{1,0:T(8,128)} %param.4) | copy-start | bytes 196612
  66.3 47.4 %all-to-all-start.1 = ((f32[32,1,2048]{2,1,0:T(1,128)}), f32[32,1,2048]{2,1,0:T(1,128)S(1)}, u32[]{:S(2)}, u32[]{:S(2)}) async-start(f32[32,1,2048]{2,1,0:T(1,128)} %reshape.69), calls=%async_computation.1 | async-start | bytes 524288 | tf_op jit(solution)/shard_map/all_to_all | solution.py:28
  304.1 50.5 %copy-start.1 = (f32[32,512]{1,0:T(8,128)}, f32[32,512]{1,0:T(8,128)S(1)}, u32[]{:S(2)}) copy-start(f32[32,512]{1,0:T(8,128)S(1)} %div.37) | copy-start | bytes 196612
  356.7 92.9 %all-to-all-start.8 = ((f32[32,1,2048]{2,1,0:T(1,128)}), f32[32,1,2048]{2,1,0:T(1,128)S(1)}, u32[]{:S(2)}, u32[]{:S(2)}) async-start(f32[32,1,2048]{2,1,0:T(1,128)} %reshape.79), calls=%async_computation.8 | async-start | bytes 524288 | tf_op jit(solution)/shard_map/all_to_all | solution.py:12
